TPU v7x, 32 devices: a whole 2x2x4 slice. The times are simulated.
32 devices in a mesh: rows: 8 (over z, y), grp: 4 (over x, core).
Axes of the slice: x: 2, y: 2, z: 4, core: 2. Of those that a mesh axis runs over, the one named last changes fastest.
Arguments:
- features: float32 [8192, 128], P(('rows', 'grp'))
- key_ids: int32 [8192], P(('rows', 'grp')), may hold values from 0 to 23, as said below
- owner: int32 [24], replicated, may hold values from 0 to 23, each once
Outputs:
- covariance: float32 [3072, 128], P(('rows', 'grp'))
Inputs may be any that keep to these rules, and one draw needn't show every extreme that they name: `key_ids`: every key is the key of at least 2 rows.
All inputs are finite; a program needn't handle non-finite values.
Results may differ from a plain program's by a relative error of at most 0.0003.
Values sent between devices are 32-bit elements; how exact they have to be, the bound alone decides.
A program may use at most 64 MiB of HBM per device.

v0:
```python
import jax
import jax.numpy as jnp
from jax import lax
from jax.sharding import PartitionSpec as P


def local(features, key_ids, owner):
    nkeys = owner.shape[0]
    width = features.shape[1]
    labels = jnp.arange(nkeys, dtype=jnp.int32)
    member = key_ids[:, None] == labels[None, :]
    slot = jnp.sum(jnp.where(member, owner[None, :], 0), axis=1)
    onehot = (slot[:, None] == labels[None, :]).astype(jnp.float32)
    contract = (((0,), (0,)), ((), ()))
    local_total = lax.dot_general(
        onehot,
        features,
        contract,
        precision=lax.Precision.HIGHEST,
        preferred_element_type=jnp.float32,
    )
    local_count = jnp.sum(onehot, axis=0)
    weighted = (onehot[:, :, None] * features[:, None, :]).reshape(features.shape[0], nkeys * width)
    gram_flat = lax.dot_general(
        weighted,
        features,
        contract,
        precision=lax.Precision.HIGHEST,
        preferred_element_type=jnp.float32,
    )
    n_rows = lax.axis_size("rows")
    n_grp = lax.axis_size("grp")
    local_rows = nkeys * width // (n_rows * n_grp)
    partial_value = lax.psum_scatter(gram_flat, "rows", scatter_dimension=0, tiled=True)
    received = lax.psum_scatter(partial_value, "grp", scatter_dimension=0, tiled=True)
    position = lax.axis_index("rows") * n_grp + lax.axis_index("grp")
    base = position * local_rows
    target = base + jnp.arange(local_rows, dtype=jnp.int32)
    owner_slot = target // width
    column = target % width
    total, count = lax.psum((local_total, local_count), ("rows", "grp"))
    slot_total = jnp.take(total, owner_slot, axis=0)
    slot_count = jnp.take(count, owner_slot, axis=0)[:, None]
    own_total = jnp.take_along_axis(slot_total, column[:, None], axis=1)
    centred = received - own_total * slot_total / slot_count
    return centred / (slot_count - 1.0)


def solution(mesh):
    placed = (P(("rows", "grp"), None), P(("rows", "grp")), P())
    return jax.shard_map(
        local, mesh=mesh, in_specs=placed, out_specs=P(("rows", "grp"), None), check_vma=False
    )
```

profile of v0, /device:TPU:0, one launch (start us, length us, event | category | flops | bytes accessed | tf_op | source)
XLA Modules:
  0.0 113.6 jit_solution(11234650140521624888)
XLA Ops:
  6.5 0.0 copy-start
  6.5 0.0 reduce-scatter.3.cloned.1.call-start
  6.5 0.8 select_reduce_fusion
  7.4 0.1 copy.4
  7.5 1.8 %broadcast_multiply_fusion = f32[256,24,128]{2,1,0:T(8,128)S(1)} fusion(f32[256,128]{1,0:T(8,128)} %param.3, f32[256,24]{1,0:T(8,128)S(1)} %copy.4), kind=kLoop, calls=%fused_computation.6 | loop fusion | flops 786432 | bytes 3301376 | tf_op jit(solution)/shard_map/mul | solution.py:23
  9.3 0.0 copy-done
  9.3 6.2 %fusion = f32[3072,128]{1,0:T(8,128)} fusion(f32[256,128]{1,0:T(8,128)S(1)} %copy-done, f32[32,8,24,128]{3,2,1,0:T(8,128)S(1)} %bitcast.12), kind=kOutput, calls=%fused_computation.3 | convolution fusion | flops 1207959552 | bytes 4849664 | tf_op jit(solution)/shard_map/dot_general | solution.py:24
  15.5 0.0 reduce-scatter.3.cloned.1.call-update
  15.5 0.0 reduce-scatter.5.cloned.1.call-start
  15.6 0.1 fusion.6
  15.7 0.2 fusion.3
  15.8 42.8 %all-reduce = (f32[24,128]{1,0:T(8,128)S(1)}, f32[24]{0:T(128)S(1)}) all-reduce(f32[24,128]{1,0:T(8,128)S(1)} %fusion.3, f32[24]{0:T(128)S(1)} %fusion.6), channel_id=1, replica_groups=mesh['rows'=8,'grp'=4] {'rows','grp'}, use_global_device_ids=true, to_apply=%region_3.4 | all-reduce | flops 3096 | bytes 24768 | tf_op jit(solution)/shard_map/psum | solution.py:41
  58.6 1.2 %gather_fusion.1 = f32[96]{0:T(128)S(1)} fusion(f32[24]{0:T(128)S(1)} %get-tuple-element.6, s32[1024]{0:T(1024)S(1)} %pad_clamp_fusion), kind=kCustom, calls=%fused_computation.1 | custom fusion | bytes 1152 | tf_op jit(solution)/shard_map/jit(_take)/gather | solution.py:43
  59.9 0.6 gather_fusion
  60.6 0.1 broadcast_select_fusion
  60.6 23.5 %reduce-scatter.3.cloned.1.call-done = f32[384,128]{1,0:T(8,128)} async-done(((f32[3072,128]{1,0:T(8,128)}), f32[384,128]{1,0:T(8,128)}) %reduce-scatter.3.cloned.1.call-update) | async-done | bytes 196624 | tf_op jit(solution)/shard_map/reduce_scatter | solution.py:34
  84.1 0.0 reduce-scatter.5.cloned.1.call-update
  84.2 1.2 %gather_fusion.2 = f32[96]{0:T(128)S(1)} fusion(f32[96,128]{1,0:T(8,128)S(1)} %broadcast_select_fusion, s32[96]{0:T(128)S(1)} %or_bitcast_fusion), kind=kCustom, calls=%fused_computation.2 | custom fusion | bytes 1536 | tf_op jit(solution)/shard_map/jit(take_along_axis)/gather | solution.py:44
  85.4 19.8 %reduce-scatter.5.cloned.1.call-done = f32[96,128]{1,0:T(8,128)} async-done(((f32[384,128]{1,0:T(8,128)}), f32[96,128]{1,0:T(8,128)}) %reduce-scatter.5.cloned.1.call-update) | async-done | bytes 49168 | tf_op jit(solution)/shard_map/reduce_scatter | solution.py:35
  105.2 1.5 %subtract_divide_fusion = f32[96,128]{1,0:T(8,128)} fusion(f32[96,128]{1,0:T(8,128)} %reduce-scatter.5.cloned.1.call-done, f32[96]{0:T(128)S(1)} %get-tuple-element.7, f32[96]{0:T(128)S(1)} %get-tuple-element.8, f32[96]{0:T(128)S(1)} %get-tuple-element.9, f32[96,128]{1,0:T(8,128)S(1)} %gather_fusion, pred[96]{0:T(512)(128)(4,1)S(1)} %compare_and_fusion), kind=kLoop, calls=%fused_computation.7 | loop fusion | flops 61440 | bytes 148704 | tf_op jit(solution)/shard_map/div | solution.py:46
  (9 shorter events, 0.1 us)
Async XLA Ops:
  6.5 2.7 %copy-start = (f32[256,128]{1,0:T(8,128)S(1)}, f32[256,128]{1,0:T(8,128)}, u32[]{:S(2)}) copy-start(f32[256,128]{1,0:T(8,128)} %param.3) | copy-start | bytes 393220
  6.5 77.6 %reduce-scatter.3.cloned.1.call-start = ((), (), s32[]{:S(2)}) async-start(), calls=%async_computation.2 | async-start | bytes 1769472 | tf_op jit(solution)/shard_map/reduce_scatter | solution.py:34
  15.5 89.7 %reduce-scatter.5.cloned.1.call-start = ((), (), s32[]{:S(2)}) async-start(), calls=%async_computation.3 | async-start | bytes 245760 | tf_op jit(solution)/shard_map/reduce_scatter | solution.py:35
Sparse Core Ops, SparseCore 0:
  15.6 68.4 reduce-scatter.2
  86.6 18.5 reduce-scatter.4
where the time goes:
time: 114 us
  waiting for transfers between devices  43.3 us (38%)
  blocking collectives  42.8 us (38%)
  between operations  13.5 us (12%)
  matrix products  6.39 us (6%)
  other arithmetic  4.42 us (4%)
  local copies, waits for them, and re-layouts  3.2 us (3%)
    psum x1, blocking collectives, local(): total, count = lax.psum((local_total, local_count), ('rows', 'grp'))  42.8 us
    reduce_scatter x1, waiting for transfers between devices, local(): lax.psum_scatter(gram_flat, 'rows', scatter_dimension=0, tiled=True)  23.5 us
    reduce_scatter x1, waiting for transfers between devices, local(): lax.psum_scatter(partial_value, 'grp', scatter_dimension=0, tiled=True)  19.8 us
    dot_general x1, matrix products, local(): lax.dot_general(weighted, features, contract, precision=lax.Precision.HIG...  6.23 us
  transfers between devices with their start and end apart: 2, of which 2 were waited for; matrix products, arithmetic and copies ran while one was open for 3% of the time, Pallas kernels for 0%

commit v1 on v0

--- a/solution.py
+++ b/solution.py
@@ -2,6 +2,11 @@
 import jax.numpy as jnp
 from jax import lax
 from jax.sharding import PartitionSpec as P
+
+
+def by_each_axis(array, first, second):
+    partial = lax.psum(array, first)
+    return lax.psum(partial, second)
 
 
 def local(features, key_ids, owner):
@@ -38,7 +43,7 @@
     target = base + jnp.arange(local_rows, dtype=jnp.int32)
     owner_slot = target // width
     column = target % width
-    total, count = lax.psum((local_total, local_count), ("rows", "grp"))
+    total, count = by_each_axis((local_total, local_count), "grp", "rows")
     slot_total = jnp.take(total, owner_slot, axis=0)
     slot_count = jnp.take(count, owner_slot, axis=0)[:, None]
     own_total = jnp.take_along_axis(slot_total, column[:, None], axis=1)

time: 114 us -> 114 us (level)
  waiting for transfers between devices: 43.3 us -> 35.6 us
  blocking collectives: 42.8 us -> 50.3 us
    reduce_scatter x1, waiting for transfers between devices: 23.5 us -> 15.8 us  [local(): lax.psum_scatter(gram_flat, 'rows', scatter_dimension=0, tiled=True)]
    psum x1 -> x2, blocking collectives: 42.8 us -> 50.3 us  [the longest x1 37.6 us: by_each_axis(): return lax.psum(partial, second)]
where the time goes in v1:
time: 114 us; the launch traced here: 113 us
  blocking collectives  50.3 us (44%)
  waiting for transfers between devices  35.6 us (31%)
  between operations  13.5 us (12%)
  matrix products  6.39 us (6%)
  other arithmetic  4.42 us (4%)
  local copies, waits for them, and re-layouts  3.2 us (3%)
    psum x1, blocking collectives, by_each_axis(): return lax.psum(partial, second)  37.6 us
    reduce_scatter x1, waiting for transfers between devices, local(): lax.psum_scatter(partial_value, 'grp', scatter_dimension=0, tiled=True)  19.7 us
    reduce_scatter x1, waiting for transfers between devices, local(): lax.psum_scatter(gram_flat, 'rows', scatter_dimension=0, tiled=True)  15.8 us
    psum x1, blocking collectives, by_each_axis(): partial = lax.psum(array, first)  12.7 us
    dot_general x1, matrix products, local(): lax.dot_general(weighted, features, contract, precision=lax.Precision.HIG...  6.23 us
  transfers between devices with their start and end apart: 2, of which 2 were waited for; matrix products, arithmetic and copies ran while one was open for 3% of the time, Pallas kernels for 0%

profile of v1, /device:TPU:0, one launch (start us, length us, event | category | flops | bytes accessed | tf_op | source)
XLA Modules:
  0.0 113.4 jit_solution(15934128024579430360)
XLA Ops:
  6.5 0.0 copy-start
  6.5 0.0 reduce-scatter.3.cloned.1.call-start
  6.5 0.8 select_reduce_fusion
  7.4 0.1 copy.4
  7.5 1.8 %broadcast_multiply_fusion = f32[256,24,128]{2,1,0:T(8,128)S(1)} fusion(f32[256,128]{1,0:T(8,128)} %param.3, f32[256,24]{1,0:T(8,128)S(1)} %copy.4), kind=kLoop, calls=%fused_computation.6 | loop fusion | flops 786432 | bytes 3301376 | tf_op jit(solution)/shard_map/mul | solution.py:28
  9.3 0.0 copy-done
  9.3 6.2 %fusion = f32[3072,128]{1,0:T(8,128)} fusion(f32[256,128]{1,0:T(8,128)S(1)} %copy-done, f32[32,8,24,128]{3,2,1,0:T(8,128)S(1)} %bitcast.12), kind=kOutput, calls=%fused_computation.3 | convolution fusion | flops 1207959552 | bytes 4849664 | tf_op jit(solution)/shard_map/dot_general | solution.py:29
  15.5 0.0 reduce-scatter.3.cloned.1.call-update
  15.5 0.0 reduce-scatter.5.cloned.1.call-start
  15.6 0.1 fusion.6
  15.7 0.2 fusion.3
  15.8 12.7 %all-reduce.1 = (f32[24,128]{1,0:T(8,128)S(1)}, f32[24]{0:T(128)S(1)}) all-reduce(f32[24,128]{1,0:T(8,128)S(1)} %fusion.3, f32[24]{0:T(128)S(1)} %fusion.6), channel_id=1, replica_groups=mesh['rows'=8,'grp'=4] {'grp'}, use_global_device_ids=true, to_apply=%region_3.4 | all-reduce | flops 3096 | bytes 24768 | tf_op jit(solution)/shard_map/psum | solution.py:8
  28.5 37.6 %all-reduce = (f32[24,128]{1,0:T(8,128)S(1)}, f32[24]{0:T(128)S(1)}) all-reduce(f32[24,128]{1,0:T(8,128)S(1)} %get-tuple-element.7, f32[24]{0:T(128)S(1)} %get-tuple-element.8), channel_id=1, replica_groups=mesh['rows'=8,'grp'=4] {'rows'}, use_global_device_ids=true, to_apply=%region_4.5 | all-reduce | flops 3096 | bytes 24768 | tf_op jit(solution)/shard_map/psum | solution.py:9
  66.2 1.2 %gather_fusion.1 = f32[96]{0:T(128)S(1)} fusion(f32[24]{0:T(128)S(1)} %get-tuple-element.6, s32[1024]{0:T(1024)S(1)} %pad_clamp_fusion), kind=kCustom, calls=%fused_computation.1 | custom fusion | bytes 1152 | tf_op jit(solution)/shard_map/jit(_take)/gather | solution.py:48
  67.4 0.6 gather_fusion
  68.1 0.1 broadcast_select_fusion
  68.2 15.8 %reduce-scatter.3.cloned.1.call-done = f32[384,128]{1,0:T(8,128)} async-done(((f32[3072,128]{1,0:T(8,128)}), f32[384,128]{1,0:T(8,128)}) %reduce-scatter.3.cloned.1.call-update) | async-done | bytes 196624 | tf_op jit(solution)/shard_map/reduce_scatter | solution.py:39
  84.0 0.0 reduce-scatter.5.cloned.1.call-update
  84.0 1.2 %gather_fusion.2 = f32[96]{0:T(128)S(1)} fusion(f32[96,128]{1,0:T(8,128)S(1)} %broadcast_select_fusion, s32[96]{0:T(128)S(1)} %or_bitcast_fusion), kind=kCustom, calls=%fused_computation.2 | custom fusion | bytes 1536 | tf_op jit(solution)/shard_map/jit(take_along_axis)/gather | solution.py:49
  85.3 19.7 %reduce-scatter.5.cloned.1.call-done = f32[96,128]{1,0:T(8,128)} async-done(((f32[384,128]{1,0:T(8,128)}), f32[96,128]{1,0:T(8,128)}) %reduce-scatter.5.cloned.1.call-update) | async-done | bytes 49168 | tf_op jit(solution)/shard_map/reduce_scatter | solution.py:40
  105.0 1.5 %subtract_divide_fusion = f32[96,128]{1,0:T(8,128)} fusion(f32[96,128]{1,0:T(8,128)} %reduce-scatter.5.cloned.1.call-done, f32[96]{0:T(128)S(1)} %get-tuple-element.9, f32[96]{0:T(128)S(1)} %get-tuple-element.10, f32[96]{0:T(128)S(1)} %get-tuple-element.11, f32[96,128]{1,0:T(8,128)S(1)} %gather_fusion, pred[96]{0:T(512)(128)(4,1)S(1)} %compare_and_fusion), kind=kLoop, calls=%fused_computation.7 | loop fusion | flops 61440 | bytes 148704 | tf_op jit(solution)/shard_map/div | solution.py:51
  (9 shorter events, 0.1 us)
Async XLA Ops:
  6.5 2.7 %copy-start = (f32[256,128]{1,0:T(8,128)S(1)}, f32[256,128]{1,0:T(8,128)}, u32[]{:S(2)}) copy-start(f32[256,128]{1,0:T(8,128)} %param.3) | copy-start | bytes 393220
  6.5 77.4 %reduce-scatter.3.cloned.1.call-start = ((), (), s32[]{:S(2)}) async-start(), calls=%async_computation.2 | async-start | bytes 1769472 | tf_op jit(solution)/shard_map/reduce_scatter | solution.py:39
  15.5 89.5 %reduce-scatter.5.cloned.1.call-start = ((), (), s32[]{:S(2)}) async-start(), calls=%async_computation.3 | async-start | bytes 245760 | tf_op jit(solution)/shard_map/reduce_scatter | solution.py:40
Sparse Core Ops, SparseCore 0:
  15.6 68.3 reduce-scatter.2
  86.4 18.5 reduce-scatter.4
